TPU v7x, 32 devices: a whole 2x2x4 slice. The times are simulated.
32 devices in a mesh: batch: 4 (over y, core), tensor: 2 (over x), latent: 4 (over z).
Axes of the slice: x: 2, y: 2, z: 4, core: 2. Of those that a mesh axis runs over, the one named last changes fastest.
Arguments:
- residual: bfloat16 [1024, 3584], P('batch', ('tensor', 'latent')), may hold values from -6 to 6
- target: bfloat16 [1024, 3584], P('batch', ('tensor', 'latent')), may hold values from -6 to 6
- encoder_weight: bfloat16 [3584, 32768], P(None, ('tensor', 'latent')), may hold values from -0.09375 to 0.09375
- encoder_bias: bfloat16 [32768], P(('tensor', 'latent')), may hold values from -0.59765625 to 0.29882812
- decoder_weight: bfloat16 [32768, 3584], P(('tensor', 'latent')), may hold values from -0.0625 to 0.0625
- decoder_bias: bfloat16 [3584], replicated, may hold values from -3 to 3
- first_gain: bfloat16 [3584], replicated, may hold values from 0.5 to 1.5
- second_gain: bfloat16 [3584], replicated, may hold values from 0.5 to 1.5
- gate_weight: bfloat16 [3584, 7168], P(None, ('tensor', 'latent')), may hold values from -0.09375 to 0.09375
- up_weight: bfloat16 [3584, 7168], P(None, ('tensor', 'latent')), may hold values from -0.09375 to 0.09375
- down_weight: bfloat16 [7168, 3584], P(('tensor', 'latent')), may hold values from -0.09375 to 0.09375
Outputs:
- encoder_grad: bfloat16 [3584, 32768], P('batch', ('tensor', 'latent'))
- decoder_grad: bfloat16 [32768, 3584], P(('tensor', 'latent'), 'batch')
All inputs are finite; a program needn't handle non-finite values.
Results may differ from a plain program's by a relative error of at most 0.012.
The roundings to bfloat16 on the way count: a program that leaves them out, or rounds other values in their place, can miss the bound.
Values may be sent and summed in bfloat16 or wider, within the bound.
A program may use at most 192 MiB of HBM per device.

v0:
```python
import jax
import jax.numpy as jnp
from jax import lax
from jax.sharding import PartitionSpec as P

epsilon = 1e-06


def per_device(
    residual,
    target,
    encoder_weight,
    encoder_bias,
    decoder_weight,
    decoder_bias,
    first_gain,
    second_gain,
    gate_weight,
    up_weight,
    down_weight,
):
    f32 = jnp.float32
    bf16 = jnp.bfloat16
    contract_last = (((1,), (1,)), ((), ()))
    contract_first = (((0,), (0,)), ((), ()))
    share_width = residual.shape[1]
    model_width = share_width * lax.axis_size(("tensor", "latent"))
    offset = lax.axis_index(("tensor", "latent")) * share_width
    token_count = residual.shape[0] * lax.axis_size("batch")
    bias_share = lax.dynamic_slice_in_dim(decoder_bias.astype(f32), offset, share_width)
    first_share = lax.dynamic_slice_in_dim(first_gain.astype(f32), offset, share_width)
    second_share = lax.dynamic_slice_in_dim(second_gain.astype(f32), offset, share_width)
    centered_share = (residual.astype(f32) - bias_share).astype(bf16)
    centered = lax.all_gather(centered_share, ("tensor", "latent"), axis=1, tiled=True)
    preact = jnp.dot(centered, encoder_weight, preferred_element_type=f32) + encoder_bias.astype(
        f32
    )
    latents = jnp.maximum(preact, 0.0).astype(bf16)
    partial_recon = jnp.dot(latents, decoder_weight, preferred_element_type=f32)
    recon_full = lax.psum(partial_recon.astype(jnp.bfloat16), ("tensor", "latent")).astype(
        jnp.float32
    ) + decoder_bias.astype(f32)
    scale_in = lax.rsqrt(
        jnp.sum(recon_full * recon_full, axis=1, keepdims=True) / model_width + epsilon
    )
    normed_input = (recon_full * scale_in * first_gain.astype(f32)).astype(bf16)
    recon = lax.dynamic_slice_in_dim(recon_full, offset, share_width, 1)
    gate_value = jnp.dot(normed_input, gate_weight, preferred_element_type=f32)
    up_value = jnp.dot(normed_input, up_weight, preferred_element_type=f32)
    gelu_value, gelu_back = jax.vjp(lambda v: jax.nn.gelu(v, approximate=True), gate_value)
    hidden = (gelu_value * up_value).astype(bf16)
    partial_out = jnp.dot(hidden, down_weight, preferred_element_type=f32)
    output = lax.psum_scatter(
        partial_out.astype(jnp.bfloat16), ("tensor", "latent"), scatter_dimension=1, tiled=True
    ).astype(jnp.float32)
    out_squares = lax.psum(jnp.sum(output * output, axis=1), ("tensor", "latent"))
    scale_out = lax.rsqrt(out_squares[:, None] / model_width + epsilon)
    normed_out = output * scale_out
    result = recon + normed_out * second_share
    grad_result = 2.0 * (result - target.astype(f32)) / token_count
    grad_normed = grad_result * second_share
    inner_out = (
        lax.psum(jnp.sum(grad_normed * normed_out, axis=1), ("tensor", "latent")) / model_width
    )
    grad_share = (scale_out * (grad_normed - normed_out * inner_out[:, None])).astype(bf16)
    grad_output = lax.all_gather(grad_share, ("tensor", "latent"), axis=1, tiled=True)
    grad_hidden = lax.dot_general(
        grad_output, down_weight, contract_last, preferred_element_type=f32
    )
    grad_gate = gelu_back(grad_hidden * up_value)[0].astype(bf16)
    grad_up = (grad_hidden * gelu_value).astype(bf16)
    partial_input = lax.dot_general(
        grad_gate, gate_weight, contract_last, preferred_element_type=f32
    )
    partial_input = partial_input + lax.dot_general(
        grad_up, up_weight, contract_last, preferred_element_type=f32
    )
    grad_normed_in = lax.psum_scatter(
        partial_input.astype(jnp.bfloat16), ("tensor", "latent"), scatter_dimension=1, tiled=True
    ).astype(jnp.float32)
    unit = recon * scale_in
    grad_unit = grad_normed_in * first_share
    inner_in = lax.psum(jnp.sum(grad_unit * unit, axis=1), ("tensor", "latent")) / model_width
    recon_share = (grad_result + scale_in * (grad_unit - unit * inner_in[:, None])).astype(bf16)
    grad_recon = lax.all_gather(recon_share, ("tensor", "latent"), axis=1, tiled=True)
    grad_latent = lax.dot_general(
        grad_recon, decoder_weight, contract_last, preferred_element_type=f32
    )
    grad_preact = jnp.where(preact > 0, grad_latent, 0.0).astype(bf16)
    centered_block, recon_block = (
        lax.all_to_all(centered, "batch", split_axis=1, concat_axis=0, tiled=True),
        lax.all_to_all(grad_recon, "batch", split_axis=1, concat_axis=0, tiled=True),
    )
    latents_all, preact_all = (
        lax.all_gather(latents, "batch", axis=0, tiled=True),
        lax.all_gather(grad_preact, "batch", axis=0, tiled=True),
    )
    encoder_grad = lax.dot_general(
        centered_block, preact_all, contract_first, preferred_element_type=f32
    )
    decoder_grad = lax.dot_general(
        latents_all, recon_block, contract_first, preferred_element_type=f32
    )
    return (encoder_grad.astype(bf16), decoder_grad.astype(bf16))


def solution(mesh):
    in_specs = (
        P("batch", ("tensor", "latent")),
        P("batch", ("tensor", "latent")),
        P(None, ("tensor", "latent")),
        P(("tensor", "latent")),
        P(("tensor", "latent"), None),
        P(),
        P(),
        P(),
        P(None, ("tensor", "latent")),
        P(None, ("tensor", "latent")),
        P(("tensor", "latent"), None),
    )
    out_specs = (P("batch", ("tensor", "latent")), P(("tensor", "latent"), "batch"))
    return jax.shard_map(
        per_device, mesh=mesh, in_specs=in_specs, out_specs=out_specs, check_vma=False
    )
```

profile of v0, /device:TPU:0, one launch (start us, length us, event | category | flops | bytes accessed | tf_op | source)
XLA Modules:
  0.0 670.3 jit_solution(1007464066563289429)
XLA Ops:
  7.2 0.0 all-gather.6.cloned.1.call-start
  7.2 0.8 dynamic_slice.12
  8.0 1.8 subtract_convert_fusion
  9.7 0.0 all-gather.6.cloned.1.call-update
  9.8 0.0 all-reduce.2.cloned.1.call-start
  9.8 0.7 convert_element_type.74
  10.5 49.3 %all-gather.6.cloned.1.call-done = bf16[256,3584]{0,1:T(8,128)(2,1)} async-done(((bf16[256,448]{0,1:T(8,128)(2,1)}), bf16[256,3584]{0,1:T(8,128)(2,1)}) %all-gather.6.cloned.1.call-update) | async-done | bytes 1835024 | tf_op jit(solution)/shard_map/all_gather | solution.py:34
  59.8 15.2 %maximum_convert_fusion = (bf16[256,4096]{1,0:T(8,128)(2,1)S(1)}, f32[256,4096]{1,0:T(8,128)}) fusion(f32[4096]{0:T(1024)S(1)} %convert_element_type.74, bf16[256,3584]{0,1:T(8,128)(2,1)} %all-gather.6.cloned.1.call-done, bf16[3584,4096]{1,0:T(8,128)(2,1)} %param.13), kind=kOutput, calls=%fused_computation.11 | convolution fusion | flops 7519338496 | bytes 37502976 | tf_op jit(solution)/shard_map/dot_general | solution.py:35
  75.0 15.5 %convolution_convert_fusion.2 = bf16[256,3584]{1,0:T(8,128)(2,1)} fusion(bf16[256,4096]{1,0:T(8,128)(2,1)S(1)} %get-tuple-element.4, bf16[4096,3584]{1,0:T(8,128)(2,1)} %param.15), kind=kOutput, calls=%fused_computation.5 | convolution fusion | flops 7517110272 | bytes 33292288 | tf_op jit(solution)/shard_map/dot_general | solution.py:39
  90.4 0.0 copy-done
  90.5 0.0 all-reduce.2.cloned.1.call-update
  90.5 0.2 reduce-scatter.7.cloned.1.call-start
  90.7 94.5 %all-reduce.2.cloned.1.call-done = bf16[256,3584]{1,0:T(8,128)(2,1)} async-done(((bf16[256,3584]{1,0:T(8,128)(2,1)}), bf16[256,3584]{1,0:T(8,128)(2,1)}) %all-reduce.2.cloned.1.call-update) | async-done | bytes 1835024 | tf_op jit(solution)/shard_map/psum | solution.py:40
  185.2 4.0 convert_add_fusion
  189.2 0.0 slice-start.4
  189.2 5.6 fusion.30
  194.9 0.0 slice-start.5
  194.9 2.1 fusion.29
  197.1 0.0 copy-start.4
  197.1 4.3 fusion.2
  201.4 0.0 reduce-scatter.7.cloned.1.call-update
  201.4 0.0 all-gather.8.cloned.1.call-start
  201.4 0.1 copy.36
  201.6 0.8 broadcast_multiply_fusion
  202.4 0.8 dynamic-slice_convert_fusion
  203.1 64.5 %reduce-scatter.7.cloned.1.call-done = bf16[448,256]{1,0:T(8,128)(2,1)} async-done(((bf16[3584,256]{1,0:T(8,128)(2,1)}), bf16[448,256]{1,0:T(8,128)(2,1)}) %reduce-scatter.7.cloned.1.call-update) | async-done | bytes 229392
  267.7 1.1 copy.42
  268.7 0.1 fusion.20
  268.9 19.4 %psum.29 = f32[256]{0:T(256)S(1)} all-reduce(f32[256]{0:T(256)S(1)} %fusion.20), channel_id=1, replica_groups=mesh['batch'=4,'tensor'=2,'latent'=4] {'tensor','latent'}, use_global_device_ids=true, to_apply=%region_4.0 | all-reduce | flops 256 | bytes 2048 | tf_op jit(solution)/shard_map/psum | solution.py:56
  288.3 1.4 fusion.16
  289.7 17.2 %psum.30 = f32[256]{0:T(256)S(1)} all-reduce(f32[256]{0:T(256)S(1)} %fusion.16), channel_id=1, replica_groups=mesh['batch'=4,'tensor'=2,'latent'=4] {'tensor','latent'}, use_global_device_ids=true, to_apply=%region_6.0 | all-reduce | flops 256 | bytes 2048 | tf_op jit(solution)/shard_map/psum | solution.py:63
  307.0 1.4 fusion.19
  308.4 0.9 copy.37
  309.2 0.0 all-gather.8.cloned.1.call-update
  309.2 0.3 reduce-scatter.9.cloned.1.call-start
  309.5 45.8 %all-gather.8.cloned.1.call-done = bf16[256,3584]{0,1:T(8,128)(2,1)} async-done(((bf16[256,448]{0,1:T(8,128)(2,1)}), bf16[256,3584]{0,1:T(8,128)(2,1)}) %all-gather.8.cloned.1.call-update) | async-done | bytes 1835024 | tf_op jit(solution)/shard_map/all_gather | solution.py:66
  355.3 5.6 fusion.45
  361.0 0.0 slice-start.3
  361.0 5.4 fusion.21
  366.5 3.6 fusion.3
  370.1 0.0 reduce-scatter.9.cloned.1.call-update
  370.1 0.0 all-gather.10.cloned.1.call-start
  370.2 0.1 dynamic_slice.15
  370.3 65.2 %reduce-scatter.9.cloned.1.call-done = bf16[448,256]{1,0:T(8,128)(2,1)} async-done(((bf16[3584,256]{1,0:T(8,128)(2,1)}), bf16[448,256]{1,0:T(8,128)(2,1)}) %reduce-scatter.9.cloned.1.call-update) | async-done | bytes 229392
  435.5 1.1 copy.44
  436.6 1.4 multiply_reduce_fusion.1
  438.0 19.3 %psum.31 = f32[256]{0:T(256)S(1)} all-reduce(f32[256]{0:T(256)S(1)} %multiply_reduce_fusion.1), channel_id=1, replica_groups=mesh['batch'=4,'tensor'=2,'latent'=4] {'tensor','latent'}, use_global_device_ids=true, to_apply=%region_9.0 | all-reduce | flops 256 | bytes 2048 | tf_op jit(solution)/shard_map/psum | solution.py:83
  457.3 1.5 add_convert_fusion
  458.8 0.8 copy.39
  459.7 0.0 all-gather.10.cloned.1.call-update
  459.7 0.0 all-gather.14.cloned.1.call-start
  459.7 0.7 all-gather.14.cloned.1.call-update
  460.4 0.0 all-gather.12.cloned.1.call-start
  460.5 44.0 %all-gather.10.cloned.1.call-done = bf16[256,3584]{0,1:T(8,128)(2,1)} async-done(((bf16[256,448]{0,1:T(8,128)(2,1)}), bf16[256,3584]{0,1:T(8,128)(2,1)}) %all-gather.10.cloned.1.call-update) | async-done | bytes 1835024 | tf_op jit(solution)/shard_map/all_gather | solution.py:85
  504.5 18.3 %fusion = bf16[256,4096]{1,0:T(8,128)(2,1)} fusion(bf16[256,3584]{0,1:T(8,128)(2,1)} %all-gather.10.cloned.1.call-done, bf16[4096,3584]{1,0:T(8,128)(2,1)} %param.15, f32[256,4096]{1,0:T(8,128)} %get-tuple-element.5), kind=kOutput, calls=%fused_computation.6 | convolution fusion | flops 7519338496 | bytes 37486592 | tf_op jit(solution)/shard_map/dot_general | solution.py:86
  522.8 0.0 all-gather.12.cloned.1.call-update
  522.8 46.2 %all_to_all.38 = bf16[256,4,896]{0,2,1:T(8,128)(2,1)} all-to-all(bf16[256,4,896]{0,2,1:T(8,128)(2,1)S(1)} %bitcast.35), channel_id=1, replica_groups=mesh['batch'=4,'tensor'=2,'latent'=4] {'batch'}, dimensions={1} | all-to-all | bytes 3670016 | tf_op jit(solution)/shard_map/all_to_all | solution.py:91
  569.0 3.8 all-to-all-start.1
  572.9 3.6 copy.34
  576.5 24.1 %all-to-all-done.1 = bf16[256,4,896]{0,2,1:T(8,128)(2,1)S(1)} async-done(((bf16[256,4,896]{0,2,1:T(8,128)(2,1)}), bf16[256,4,896]{0,2,1:T(8,128)(2,1)S(1)}, u32[]{:S(2)}, u32[]{:S(2)}) %all-to-all-start.1) | async-done | bytes 1835040 | tf_op jit(solution)/shard_map/all_to_all | solution.py:92
  600.6 2.4 copy.40
  603.0 15.2 %convolution_convert_fusion = bf16[4096,896]{1,0:T(8,128)(2,1)} fusion(bf16[1024,4096]{1,0:T(8,128)(2,1)} %all-gather.14.cloned.1.call-done, bf16[1024,896]{1,0:T(8,128)(2,1)} %bitcast.38), kind=kOutput, calls=%fused_computation | convolution fusion | flops 7519862784 | bytes 17563648 | tf_op jit(solution)/shard_map/dot_general | solution.py:101
  618.1 33.3 %all-gather.12.cloned.1.call-done = bf16[1024,4096]{1,0:T(8,128)(2,1)} async-done(((bf16[256,4096]{1,0:T(8,128)(2,1)}), bf16[1024,4096]{1,0:T(8,128)(2,1)}) %all-gather.12.cloned.1.call-update) | async-done | bytes 8388624 | tf_op jit(solution)/shard_map/all_gather | solution.py:96
  651.4 12.1 %convolution_convert_fusion.1 = bf16[896,4096]{1,0:T(8,128)(2,1)} fusion(bf16[1024,896]{1,0:T(8,128)(2,1)S(1)} %bitcast.37, bf16[1024,4096]{1,0:T(8,128)(2,1)} %all-gather.12.cloned.1.call-done), kind=kOutput, calls=%fused_computation.1 | convolution fusion | flops 7519862784 | bytes 17563648 | tf_op jit(solution)/shard_map/dot_general | solution.py:98
  (31 shorter events, 0.1 us)
Async XLA Ops:
  7.2 52.6 %all-gather.6.cloned.1.call-start = ((), (), s32[]{:S(2)}) async-start(), calls=%async_computation.4 | async-start | bytes 2064384 | tf_op jit(solution)/shard_map/all_gather | solution.py:34
  9.8 175.5 %all-reduce.2.cloned.1.call-start = ((), (), s32[]{:S(2)}) async-start(), calls=%async_computation.5 | async-start | bytes 3670016 | tf_op jit(solution)/shard_map/psum | solution.py:40
  75.0 15.5 %copy-start = (bf16[256,4096]{1,0:T(8,128)(2,1)}, bf16[256,4096]{1,0:T(8,128)(2,1)S(1)}, u32[]{:S(2)}) copy-start(bf16[256,4096]{1,0:T(8,128)(2,1)S(1)} %get-tuple-element.4) | copy-start | bytes 6291460
  75.0 15.8 %copy-start.5 = (bf16[3584]{0:T(1024)(128)(2,1)S(1)}, bf16[3584]{0:T(1024)(128)(2,1)}, u32[]{:S(2)}) copy-start(bf16[3584]{0:T(1024)(128)(2,1)} %param.16) | copy-start | bytes 21508
  75.0 15.8 %copy-start.6 = (bf16[3584]{0:T(1024)(128)(2,1)S(1)}, bf16[3584]{0:T(1024)(128)(2,1)}, u32[]{:S(2)}) copy-start(bf16[3584]{0:T(1024)(128)(2,1)} %param.17) | copy-start | bytes 21508
  90.5 177.2 %reduce-scatter.7.cloned.1.call-start = ((), (), s32[]{:S(2)}) async-start(), calls=%async_computation.10 | async-start | bytes 2064384
  185.2 9.6 %slice-start = ((s8[6422528]{0:T(1024)(128)(4,1)}), s8[4194304]{0:T(1024)(128)(4,1)S(1)}, s32[]{:S(2)}) async-start(s8[6422528]{0:T(1024)(128)(4,1)} %bitcast.29), calls=%async_computation.12 | async-start | bytes 8388608
  189.2 5.7 slice-start.1
  189.2 5.7 copy-start.3
  189.2 7.9 %slice-start.4 = ((s8[6422528]{0:T(1024)(128)(4,1)}), s8[4194304]{0:T(1024)(128)(4,1)S(1)}, s32[]{:S(2)}) async-start(s8[6422528]{0:T(1024)(128)(4,1)} %bitcast.41), calls=%async_computation.16 | async-start | bytes 8388608
  194.9 2.2 slice-start.5
  197.1 4.4 copy-start.4
  201.4 154.0 %all-gather.8.cloned.1.call-start = ((), (), s32[]{:S(2)}) async-start(), calls=%async_computation.6 | async-start | bytes 2064384 | tf_op jit(solution)/shard_map/all_gather | solution.py:66
  309.2 126.3 %reduce-scatter.9.cloned.1.call-start = ((), (), s32[]{:S(2)}) async-start(), calls=%async_computation.11 | async-start | bytes 2064384
  355.3 11.1 %slice-start.2 = ((s8[6422528]{0:T(1024)(128)(4,1)}), s8[2228224]{0:T(1024)(128)(4,1)S(1)}, s32[]{:S(2)}) async-start(s8[6422528]{0:T(1024)(128)(4,1)} %bitcast.31), calls=%async_computation.14 | async-start | bytes 4456448
  361.0 5.5 slice-start.3
  370.1 134.3 %all-gather.10.cloned.1.call-start = ((), (), s32[]{:S(2)}) async-start(), calls=%async_computation.7 | async-start | bytes 2064384 | tf_op jit(solution)/shard_map/all_gather | solution.py:85
  459.7 143.3 %all-gather.14.cloned.1.call-start = ((), (), s32[]{:S(2)}) async-start(), calls=%async_computation.9 | async-start | bytes 10485760 | tf_op jit(solution)/shard_map/all_gather | solution.py:95
  460.4 191.0 %all-gather.12.cloned.1.call-start = ((), (), s32[]{:S(2)}) async-start(), calls=%async_computation.8 | async-start | bytes 10485760 | tf_op jit(solution)/shard_map/all_gather | solution.py:96
  504.5 18.4 %copy-start.1 = (bf16[256,3584]{0,1:T(8,128)(2,1)S(1)}, bf16[256,3584]{0,1:T(8,128)(2,1)}, u32[]{:S(2)}) copy-start(bf16[256,3584]{0,1:T(8,128)(2,1)} %all-gather.6.cloned.1.call-done) | copy-start | bytes 5505028
  569.0 31.6 %all-to-all-start.1 = ((bf16[256,4,896]{0,2,1:T(8,128)(2,1)}), bf16[256,4,896]{0,2,1:T(8,128)(2,1)S(1)}, u32[]{:S(2)}, u32[]{:S(2)}) async-start(bf16[256,4,896]{0,2,1:T(8,128)(2,1)} %bitcast.36), calls=%async_computation.1 | async-start | bytes 3670016 | tf_op jit(solution)/shard_map/all_to_all | solution.py:92
  603.0 48.5 %copy-start.2 = (bf16[4,256,896]{2,1,0:T(8,128)(2,1)S(1)}, bf16[4,256,896]{2,1,0:T(8,128)(2,1)}, u32[]{:S(2)}) copy-start(bf16[4,256,896]{2,1,0:T(8,128)(2,1)} %copy.34) | copy-start | bytes 5505028
Sparse Core Ops, SparseCore 0:
  10.6 49.1 all-gather.5
  90.6 94.5 all-reduce.1
  201.5 66.1 reduce-scatter.6
  309.4 45.9 all-gather.7
  370.3 65.1 reduce-scatter.8
  459.8 44.6 all-gather.9
  506.0 81.8 all-gather.13
  590.1 61.2 all-gather.11
where the time goes:
time: 671 us; the launch traced here: 670 us
  waiting for transfers between devices  422 us (63%)
  matrix products  103 us (15%)
  blocking collectives  102 us (15%)
  between operations  14.4 us (2%)
  other arithmetic  13.9 us (2%)
  local copies, waits for them, and re-layouts  10.9 us (2%)
    unnamed x10, waiting for transfers between devices  131 us
    psum x1, waiting for transfers between devices, per_device(): lax.psum(partial_recon.astype(jnp.bfloat16), ('tensor', 'latent'))  94.5 us
    all_gather x1, waiting for transfers between devices, per_device(): lax.all_gather(centered_share, ('tensor', 'latent'), axis=1, tiled=True)  49.3 us
    all_to_all x1, blocking collectives, per_device(): lax.all_to_all(centered, 'batch', split_axis=1, concat_axis=0, tiled=True)  46.2 us
    all_gather x1, waiting for transfers between devices, per_device(): lax.all_gather(grad_share, ('tensor', 'latent'), axis=1, tiled=True)  45.8 us
    all_gather x1, waiting for transfers between devices, per_device(): lax.all_gather(recon_share, ('tensor', 'latent'), axis=1, tiled=True)  44 us
    all_gather x1, waiting for transfers between devices, per_device(): lax.all_gather(grad_preact, 'batch', axis=0, tiled=True)  33.3 us
    all_to_all x1, waiting for transfers between devices, per_device(): lax.all_to_all(grad_recon, 'batch', split_axis=1, concat_axis=0, tiled=True)  24.1 us
  transfers between devices with their start and end apart: 9, of which 8 were waited for; matrix products, arithmetic and copies ran while one was open for 6% of the time, Pallas kernels for 0%

commit v1 on v0

--- a/solution.py
+++ b/solution.py
@@ -37,7 +37,7 @@
     )
     latents = jnp.maximum(preact, 0.0).astype(bf16)
     partial_recon = jnp.dot(latents, decoder_weight, preferred_element_type=f32)
-    recon_full = lax.psum(partial_recon.astype(jnp.bfloat16), ("tensor", "latent")).astype(
+    recon_full = lax.psum(lax.psum(partial_recon.astype(jnp.bfloat16), "tensor"), "latent").astype(
         jnp.float32
     ) + decoder_bias.astype(f32)
     scale_in = lax.rsqrt(

time: 671 us -> 712 us (1.061)
  waiting for transfers between devices: 422 us -> 463 us
    psum x1 -> x2, waiting for transfers between devices: 94.5 us -> 136 us  [the longest x1 79.7 us: per_device(): lax.psum(lax.psum(partial_recon.astype(jnp.bfloat16), 'tensor'), 'latent')]
    unnamed x10 -> x11, waiting for transfers between devices: 131 us -> 130 us
  transfers between devices with their start and end apart: 9 -> 10, of which waited for: 8 -> 9; matrix products, arithmetic and copies ran while one was open for 6% -> 6% of each run, Pallas kernels for 0% -> 0%
where the time goes in v1:
time: 712 us; the launch traced here: 711 us
  waiting for transfers between devices  463 us (65%)
  matrix products  103 us (14%)
  blocking collectives  102 us (14%)
  between operations  14.1 us (2%)
  other arithmetic  13.9 us (2%)
  local copies, waits for them, and re-layouts  10.9 us (2%)
    unnamed x11, waiting for transfers between devices  130 us
    psum x1, waiting for transfers between devices, per_device(): lax.psum(lax.psum(partial_recon.astype(jnp.bfloat16), 'tensor'), 'latent')  79.7 us
    psum x1, waiting for transfers between devices, per_device(): lax.psum(partial_recon.astype(jnp.bfloat16), 'tensor')  56.1 us
    all_gather x1, waiting for transfers between devices, per_device(): lax.all_gather(centered_share, ('tensor', 'latent'), axis=1, tiled=True)  49.3 us
    all_to_all x1, blocking collectives, per_device(): lax.all_to_all(centered, 'batch', split_axis=1, concat_axis=0, tiled=True)  46.2 us
    all_gather x1, waiting for transfers between devices, per_device(): lax.all_gather(grad_share, ('tensor', 'latent'), axis=1, tiled=True)  45.8 us
    all_gather x1, waiting for transfers between devices, per_device(): lax.all_gather(recon_share, ('tensor', 'latent'), axis=1, tiled=True)  43.9 us
    all_gather x1, waiting for transfers between devices, per_device(): lax.all_gather(grad_preact, 'batch', axis=0, tiled=True)  33.3 us
  transfers between devices with their start and end apart: 10, of which 9 were waited for; matrix products, arithmetic and copies ran while one was open for 6% of the time, Pallas kernels for 0%

profile of v1, /device:TPU:0, one launch (start us, length us, event | category | flops | bytes accessed | tf_op | source)
XLA Modules:
  0.0 711.0 jit_solution(17441820619323511569)
XLA Ops:
  7.2 0.0 all-gather.6.cloned.1.call-start
  7.2 0.8 dynamic_slice.12
  8.0 1.8 subtract_convert_fusion
  9.7 0.0 all-gather.6.cloned.1.call-update
  9.8 0.0 all-reduce.3.cloned.1.call-start
  9.8 0.7 convert_element_type.74
  10.5 49.3 %all-gather.6.cloned.1.call-done = bf16[256,3584]{0,1:T(8,128)(2,1)} async-done(((bf16[256,448]{0,1:T(8,128)(2,1)}), bf16[256,3584]{0,1:T(8,128)(2,1)}) %all-gather.6.cloned.1.call-update) | async-done | bytes 1835024 | tf_op jit(solution)/shard_map/all_gather | solution.py:34
  59.8 15.2 %maximum_convert_fusion = (bf16[256,4096]{1,0:T(8,128)(2,1)S(1)}, f32[256,4096]{1,0:T(8,128)}) fusion(f32[4096]{0:T(1024)S(1)} %convert_element_type.74, bf16[256,3584]{0,1:T(8,128)(2,1)} %all-gather.6.cloned.1.call-done, bf16[3584,4096]{1,0:T(8,128)(2,1)} %param.13), kind=kOutput, calls=%fused_computation.11 | convolution fusion | flops 7519338496 | bytes 37502976 | tf_op jit(solution)/shard_map/dot_general | solution.py:35
  75.0 15.5 %convolution_convert_fusion.2 = bf16[256,3584]{1,0:T(8,128)(2,1)} fusion(bf16[256,4096]{1,0:T(8,128)(2,1)S(1)} %get-tuple-element.4, bf16[4096,3584]{1,0:T(8,128)(2,1)} %param.15), kind=kOutput, calls=%fused_computation.5 | convolution fusion | flops 7517110272 | bytes 33292288 | tf_op jit(solution)/shard_map/dot_general | solution.py:39
  90.4 0.0 all-reduce.3.cloned.1.call-update
  90.4 0.0 all-reduce.5.cloned.1.call-start
  90.5 56.1 %all-reduce.3.cloned.1.call-done = bf16[256,3584]{1,0:T(8,128)(2,1)} async-done(((bf16[256,3584]{1,0:T(8,128)(2,1)}), bf16[256,3584]{1,0:T(8,128)(2,1)}) %all-reduce.3.cloned.1.call-update) | async-done | bytes 1835024 | tf_op jit(solution)/shard_map/psum | solution.py:40
  146.6 0.0 all-reduce.5.cloned.1.call-update
  146.6 0.2 reduce-scatter.7.cloned.1.call-start
  146.9 79.7 %all-reduce.5.cloned.1.call-done = bf16[256,3584]{1,0:T(8,128)(2,1)} async-done(((bf16[256,3584]{1,0:T(8,128)(2,1)}), bf16[256,3584]{1,0:T(8,128)(2,1)}) %all-reduce.5.cloned.1.call-update) | async-done | bytes 1835024 | tf_op jit(solution)/shard_map/psum | solution.py:40
  226.6 4.0 convert_add_fusion
  230.6 5.6 fusion.30
  236.3 0.0 slice-start.5
  236.3 2.1 fusion.29
  238.5 4.3 fusion.2
  242.8 0.0 reduce-scatter.7.cloned.1.call-update
  242.8 0.0 all-gather.8.cloned.1.call-start
  242.8 0.1 copy.36
  243.0 0.8 broadcast_multiply_fusion
  243.8 0.8 dynamic-slice_convert_fusion
  244.5 64.1 %reduce-scatter.7.cloned.1.call-done = bf16[448,256]{1,0:T(8,128)(2,1)} async-done(((bf16[3584,256]{1,0:T(8,128)(2,1)}), bf16[448,256]{1,0:T(8,128)(2,1)}) %reduce-scatter.7.cloned.1.call-update) | async-done | bytes 229392
  308.6 1.1 copy.42
  309.7 0.1 fusion.20
  309.8 19.4 %psum.37 = f32[256]{0:T(256)S(1)} all-reduce(f32[256]{0:T(256)S(1)} %fusion.20), channel_id=1, replica_groups=mesh['batch'=4,'tensor'=2,'latent'=4] {'tensor','latent'}, use_global_device_ids=true, to_apply=%region_5.0 | all-reduce | flops 256 | bytes 2048 | tf_op jit(solution)/shard_map/psum | solution.py:56
  329.2 1.4 fusion.16
  330.7 17.2 %psum.38 = f32[256]{0:T(256)S(1)} all-reduce(f32[256]{0:T(256)S(1)} %fusion.16), channel_id=1, replica_groups=mesh['batch'=4,'tensor'=2,'latent'=4] {'tensor','latent'}, use_global_device_ids=true, to_apply=%region_7.0 | all-reduce | flops 256 | bytes 2048 | tf_op jit(solution)/shard_map/psum | solution.py:63
  347.9 1.4 fusion.19
  349.3 0.9 copy.37
  350.1 0.0 all-gather.8.cloned.1.call-update
  350.2 0.3 reduce-scatter.9.cloned.1.call-start
  350.4 45.8 %all-gather.8.cloned.1.call-done = bf16[256,3584]{0,1:T(8,128)(2,1)} async-done(((bf16[256,448]{0,1:T(8,128)(2,1)}), bf16[256,3584]{0,1:T(8,128)(2,1)}) %all-gather.8.cloned.1.call-update) | async-done | bytes 1835024 | tf_op jit(solution)/shard_map/all_gather | solution.py:66
  396.3 5.6 fusion.45
  401.9 0.0 slice-start.3
  401.9 5.5 fusion.21
  407.4 3.6 fusion.3
  411.1 0.0 reduce-scatter.9.cloned.1.call-update
  411.1 0.0 all-gather.10.cloned.1.call-start
  411.1 0.1 dynamic_slice.15
  411.2 65.5 %reduce-scatter.9.cloned.1.call-done = bf16[448,256]{1,0:T(8,128)(2,1)} async-done(((bf16[3584,256]{1,0:T(8,128)(2,1)}), bf16[448,256]{1,0:T(8,128)(2,1)}) %reduce-scatter.9.cloned.1.call-update) | async-done | bytes 229392
  476.7 1.1 copy.44
  477.8 1.4 multiply_reduce_fusion.1
  479.2 19.2 %psum.39 = f32[256]{0:T(256)S(1)} all-reduce(f32[256]{0:T(256)S(1)} %multiply_reduce_fusion.1), channel_id=1, replica_groups=mesh['batch'=4,'tensor'=2,'latent'=4] {'tensor','latent'}, use_global_device_ids=true, to_apply=%region_10.0 | all-reduce | flops 256 | bytes 2048 | tf_op jit(solution)/shard_map/psum | solution.py:83
  498.4 1.5 add_convert_fusion
  500.0 0.8 copy.39
  500.8 0.0 all-gather.10.cloned.1.call-update
  500.8 0.0 all-gather.14.cloned.1.call-start
  500.9 0.7 all-gather.14.cloned.1.call-update
  501.6 0.0 all-gather.12.cloned.1.call-start
  501.6 43.9 %all-gather.10.cloned.1.call-done = bf16[256,3584]{0,1:T(8,128)(2,1)} async-done(((bf16[256,448]{0,1:T(8,128)(2,1)}), bf16[256,3584]{0,1:T(8,128)(2,1)}) %all-gather.10.cloned.1.call-update) | async-done | bytes 1835024 | tf_op jit(solution)/shard_map/all_gather | solution.py:85
  545.5 18.3 %fusion = bf16[256,4096]{1,0:T(8,128)(2,1)} fusion(bf16[256,3584]{0,1:T(8,128)(2,1)} %all-gather.10.cloned.1.call-done, bf16[4096,3584]{1,0:T(8,128)(2,1)} %param.15, f32[256,4096]{1,0:T(8,128)} %get-tuple-element.5), kind=kOutput, calls=%fused_computation.6 | convolution fusion | flops 7519338496 | bytes 37486592 | tf_op jit(solution)/shard_map/dot_general | solution.py:86
  563.8 0.0 all-gather.12.cloned.1.call-update
  563.8 46.2 %all_to_all.38 = bf16[256,4,896]{0,2,1:T(8,128)(2,1)} all-to-all(bf16[256,4,896]{0,2,1:T(8,128)(2,1)S(1)} %bitcast.35), channel_id=1, replica_groups=mesh['batch'=4,'tensor'=2,'latent'=4] {'batch'}, dimensions={1} | all-to-all | bytes 3670016 | tf_op jit(solution)/shard_map/all_to_all | solution.py:91
  610.0 3.8 all-to-all-start.1
  613.9 3.6 copy.34
  617.5 24.1 %all-to-all-done.1 = bf16[256,4,896]{0,2,1:T(8,128)(2,1)S(1)} async-done(((bf16[256,4,896]{0,2,1:T(8,128)(2,1)}), bf16[256,4,896]{0,2,1:T(8,128)(2,1)S(1)}, u32[]{:S(2)}, u32[]{:S(2)}) %all-to-all-start.1) | async-done | bytes 1835040 | tf_op jit(solution)/shard_map/all_to_all | solution.py:92
  641.6 2.4 copy.40
  644.0 15.2 %convolution_convert_fusion = bf16[4096,896]{1,0:T(8,128)(2,1)} fusion(bf16[1024,4096]{1,0:T(8,128)(2,1)} %all-gather.14.cloned.1.call-done, bf16[1024,896]{1,0:T(8,128)(2,1)} %bitcast.38), kind=kOutput, calls=%fused_computation | convolution fusion | flops 7519862784 | bytes 17563648 | tf_op jit(solution)/shard_map/dot_general | solution.py:101
  659.1 33.3 %all-gather.12.cloned.1.call-done = bf16[1024,4096]{1,0:T(8,128)(2,1)} async-done(((bf16[256,4096]{1,0:T(8,128)(2,1)}), bf16[1024,4096]{1,0:T(8,128)(2,1)}) %all-gather.12.cloned.1.call-update) | async-done | bytes 8388624 | tf_op jit(solution)/shard_map/all_gather | solution.py:96
  692.4 12.1 %convolution_convert_fusion.1 = bf16[896,4096]{1,0:T(8,128)(2,1)} fusion(bf16[1024,896]{1,0:T(8,128)(2,1)S(1)} %bitcast.37, bf16[1024,4096]{1,0:T(8,128)(2,1)} %all-gather.12.cloned.1.call-done), kind=kOutput, calls=%fused_computation.1 | convolution fusion | flops 7519862784 | bytes 17563648 | tf_op jit(solution)/shard_map/dot_general | solution.py:98
  (34 shorter events, 0.1 us)
Async XLA Ops:
  7.2 52.6 %all-gather.6.cloned.1.call-start = ((), (), s32[]{:S(2)}) async-start(), calls=%async_computation.4 | async-start | bytes 2064384 | tf_op jit(solution)/shard_map/all_gather | solution.py:34
  9.8 136.8 %all-reduce.3.cloned.1.call-start = ((), (), s32[]{:S(2)}) async-start(), calls=%async_computation.5 | async-start | bytes 3670016 | tf_op jit(solution)/shard_map/psum | solution.py:40
  75.0 15.5 %copy-start = (bf16[256,4096]{1,0:T(8,128)(2,1)}, bf16[256,4096]{1,0:T(8,128)(2,1)S(1)}, u32[]{:S(2)}) copy-start(bf16[256,4096]{1,0:T(8,128)(2,1)S(1)} %get-tuple-element.4) | copy-start | bytes 6291460
  90.4 56.4 %copy-start.5 = (bf16[3584]{0:T(1024)(128)(2,1)S(1)}, bf16[3584]{0:T(1024)(128)(2,1)}, u32[]{:S(2)}) copy-start(bf16[3584]{0:T(1024)(128)(2,1)} %param.16) | copy-start | bytes 21508
  90.4 56.4 %copy-start.6 = (bf16[3584]{0:T(1024)(128)(2,1)S(1)}, bf16[3584]{0:T(1024)(128)(2,1)}, u32[]{:S(2)}) copy-start(bf16[3584]{0:T(1024)(128)(2,1)} %param.17) | copy-start | bytes 21508
  90.4 136.2 %all-reduce.5.cloned.1.call-start = ((), (), s32[]{:S(2)}) async-start(), calls=%async_computation.6 | async-start | bytes 3670016 | tf_op jit(solution)/shard_map/psum | solution.py:40
  146.6 162.0 %reduce-scatter.7.cloned.1.call-start = ((), (), s32[]{:S(2)}) async-start(), calls=%async_computation.11 | async-start | bytes 2064384
  226.6 9.6 %slice-start = ((s8[6422528]{0:T(1024)(128)(4,1)}), s8[4194304]{0:T(1024)(128)(4,1)S(1)}, s32[]{:S(2)}) async-start(s8[6422528]{0:T(1024)(128)(4,1)} %bitcast.29), calls=%async_computation.13 | async-start | bytes 8388608
  230.6 5.7 slice-start.1
  230.6 5.7 copy-start.3
  230.6 7.9 %slice-start.4 = ((s8[6422528]{0:T(1024)(128)(4,1)}), s8[4194304]{0:T(1024)(128)(4,1)S(1)}, s32[]{:S(2)}) async-start(s8[6422528]{0:T(1024)(128)(4,1)} %bitcast.41), calls=%async_computation.17 | async-start | bytes 8388608
  236.3 2.2 slice-start.5
  238.5 4.4 copy-start.4
  242.8 153.5 %all-gather.8.cloned.1.call-start = ((), (), s32[]{:S(2)}) async-start(), calls=%async_computation.7 | async-start | bytes 2064384 | tf_op jit(solution)/shard_map/all_gather | solution.py:66
  350.2 126.5 %reduce-scatter.9.cloned.1.call-start = ((), (), s32[]{:S(2)}) async-start(), calls=%async_computation.12 | async-start | bytes 2064384
  396.3 11.1 %slice-start.2 = ((s8[6422528]{0:T(1024)(128)(4,1)}), s8[2228224]{0:T(1024)(128)(4,1)S(1)}, s32[]{:S(2)}) async-start(s8[6422528]{0:T(1024)(128)(4,1)} %bitcast.31), calls=%async_computation.15 | async-start | bytes 4456448
  401.9 5.5 slice-start.3
  411.1 134.4 %all-gather.10.cloned.1.call-start = ((), (), s32[]{:S(2)}) async-start(), calls=%async_computation.8 | async-start | bytes 2064384 | tf_op jit(solution)/shard_map/all_gather | solution.py:85
  500.8 143.2 %all-gather.14.cloned.1.call-start = ((), (), s32[]{:S(2)}) async-start(), calls=%async_computation.10 | async-start | bytes 10485760 | tf_op jit(solution)/shard_map/all_gather | solution.py:95
  501.6 190.9 %all-gather.12.cloned.1.call-start = ((), (), s32[]{:S(2)}) async-start(), calls=%async_computation.9 | async-start | bytes 10485760 | tf_op jit(solution)/shard_map/all_gather | solution.py:96
  545.5 18.4 %copy-start.1 = (bf16[256,3584]{0,1:T(8,128)(2,1)S(1)}, bf16[256,3584]{0,1:T(8,128)(2,1)}, u32[]{:S(2)}) copy-start(bf16[256,3584]{0,1:T(8,128)(2,1)} %all-gather.6.cloned.1.call-done) | copy-start | bytes 5505028
  610.0 31.6 %all-to-all-start.1 = ((bf16[256,4,896]{0,2,1:T(8,128)(2,1)}), bf16[256,4,896]{0,2,1:T(8,128)(2,1)S(1)}, u32[]{:S(2)}, u32[]{:S(2)}) async-start(bf16[256,4,896]{0,2,1:T(8,128)(2,1)} %bitcast.36), calls=%async_computation.1 | async-start | bytes 3670016 | tf_op jit(solution)/shard_map/all_to_all | solution.py:92
  644.0 48.5 %copy-start.2 = (bf16[4,256,896]{2,1,0:T(8,128)(2,1)S(1)}, bf16[4,256,896]{2,1,0:T(8,128)(2,1)}, u32[]{:S(2)}) copy-start(bf16[4,256,896]{2,1,0:T(8,128)(2,1)} %copy.34) | copy-start | bytes 5505028
Sparse Core Ops, SparseCore 0:
  10.6 49.1 all-gather.5
  90.6 55.9 all-reduce.2
  149.0 77.6 all-reduce.4
  242.9 65.6 reduce-scatter.6
  350.3 45.9 all-gather.7
  411.2 65.4 reduce-scatter.8
  500.9 44.5 all-gather.9
  547.0 81.8 all-gather.13
  631.1 61.3 all-gather.11
